TPU v7x, 128 devices: a whole 4x4x4 slice. The times are simulated.
128 devices in a mesh: group: 32 (over z, y, core), local: 4 (over x).
Axes of the slice: x: 4, y: 4, z: 4, core: 2. Of those that a mesh axis runs over, the one named last changes fastest.
Arguments:
- dense_vec: bfloat16 [16384, 128], P(('group', 'local')), may hold values from -6 to 6
- q_tables: float32 [4096, 26, 128], P('group'), may hold values from -4 to 4
- r_tables: float32 [256, 26, 128], P('local'), may hold values from -4 to 4
- owner: int32 [16384, 26, 1], P(('group', 'local')), may hold values from 0 to 31; in each aligned block of 3328 rows (0 to 3327, 3328 to 6655, ..., all dimensions but the last counted through in order) at most 208 rows name the same one
- q_local: int32 [16384, 26], P(('group', 'local')), may hold values from 0 to 127
- r_index: int32 [16384, 26], P(('group', 'local')), may hold values from 0 to 255
- w_one: bfloat16 [479, 1024], replicated, may hold values from -0.25 to 0.25
- b_one: float32 [1024], replicated, may hold values from -3 to 3
- w_two: bfloat16 [1024, 1024], replicated, may hold values from -0.1875 to 0.1875
- b_two: float32 [1024], replicated, may hold values from -3 to 3
- w_three: bfloat16 [1024, 512], replicated, may hold values from -0.1875 to 0.1875
- b_three: float32 [512], replicated, may hold values from -3 to 3
- w_four: bfloat16 [512, 256], replicated, may hold values from -0.25 to 0.25
- b_four: float32 [256], replicated, may hold values from -3 to 3
- cotangent: bfloat16 [16384, 256], P(('group', 'local')), may hold values from -6 to 6
Outputs:
- q_new: float32 [4096, 26, 128], P('group')
- r_new: float32 [256, 26, 128], P('local')
- w_one_new: float32 [479, 1024], replicated
- b_one_new: float32 [1024], replicated
- w_two_new: float32 [1024, 1024], replicated
- b_two_new: float32 [1024], replicated
- w_three_new: float32 [1024, 512], replicated
- b_three_new: float32 [512], replicated
- w_four_new: float32 [512, 256], replicated
- b_four_new: float32 [256], replicated
Inputs may be any that keep to these rules, and one draw needn't show every extreme that they name: `owner`: within the rows of one device (its 128 samples times 26 tables), no group is named more than 208 times, a bound that some block reaches.
All inputs are finite; a program needn't handle non-finite values.
Results may differ from a plain program's by a relative error of at most 0.0025.
Values may be sent and summed in bfloat16 or wider, within the bound.
No kernel may reach another device: no remote copies, remote signals or barrier semaphores. Data moves between devices by JAX's collectives and lax.ppermute only.
A program may use at most 128 MiB of HBM per device.

v0:
```python
import jax
import jax.numpy as jnp
import numpy as np
from jax import lax
from jax.sharding import PartitionSpec as P

table_rate = 0.05
dense_rate = 0.0005


def cut_along(array, dim, length):
    before, after = (array.shape[:dim], array.shape[dim + 1 :])
    return jnp.moveaxis(array.reshape(*before, length, -1, *after), dim, 0)


def summed_on_arrival(array, axis, dim):
    blocks = cut_along(array, dim, lax.axis_size(axis))
    arrived = lax.all_to_all(blocks, axis, split_axis=0, concat_axis=0, tiled=True)
    return arrived.astype(jnp.float32).sum(axis=0)


def in_order(blocks, dim):
    shape = list(blocks.shape[1:])
    shape[dim] *= blocks.shape[0]
    return jnp.moveaxis(blocks, 0, dim).reshape(shape)


def sent_to_all(array, axis):
    length = lax.axis_size(axis)
    return lax.all_to_all(
        jnp.broadcast_to(array[None], (length, *array.shape)), axis, 0, 0, tiled=True
    )


def gather_directly(array, axis, dim):
    return in_order(sent_to_all(array, axis), dim)


def silu_slope(preact):
    sigma = jax.nn.sigmoid(preact)
    return sigma * (1.0 + preact * (1.0 - sigma))


def interact(dense_rows, embeds):
    vectors_all = jnp.concatenate([dense_rows[:, None, :], embeds], axis=1).astype(jnp.float32)
    gram_mat = jnp.einsum("bid,bjd->bij", vectors_all, vectors_all, precision=lax.Precision.HIGHEST)
    lower_i, lower_j = np.tril_indices(vectors_all.shape[1], -1)
    pair_vals = gram_mat[:, lower_i, lower_j]
    features = jnp.concatenate([dense_rows.astype(jnp.float32), pair_vals], axis=1).astype(
        jnp.bfloat16
    )
    return (vectors_all, features)


def pair_back(d_pairs, vectors_all):
    vectors = vectors_all.shape[1]
    lower_i, lower_j = np.tril_indices(vectors, -1)
    spread = (
        jnp.zeros((vectors_all.shape[0], vectors, vectors), jnp.float32)
        .at[:, lower_i, lower_j]
        .set(d_pairs)
    )
    spread = spread + jnp.swapaxes(spread, 1, 2)
    return jnp.einsum("bij,bjd->bid", spread, vectors_all, precision=lax.Precision.HIGHEST)


def contract_rows(left, right):
    return lax.dot_general(
        left, right, (((0,), (0,)), ((), ())), preferred_element_type=jnp.float32
    )


def dense_pass(features, layers, cot_rows):
    inputs_list = [features]
    pre_list = []
    current = features
    for layer_idx, (weight, biases) in enumerate(layers):
        pre_act = jnp.dot(current, weight, preferred_element_type=jnp.float32) + biases
        pre_list.append(pre_act)
        if layer_idx + 1 < len(layers):
            current = jax.nn.silu(pre_act).astype(jnp.bfloat16)
            inputs_list.append(current)
    grad_low = cot_rows
    grad_full = cot_rows.astype(jnp.float32)
    grads = []
    back_grad = None
    for layer_idx in reversed(range(len(layers))):
        weight = layers[layer_idx][0]
        w_grad = contract_rows(inputs_list[layer_idx], grad_low)
        b_grad = jnp.sum(grad_full, axis=0)
        back_grad = lax.dot_general(
            grad_low, weight, (((1,), (1,)), ((), ())), preferred_element_type=jnp.float32
        )
        grads.insert(0, (w_grad, b_grad))
        if layer_idx > 0:
            grad_full = back_grad * silu_slope(pre_list[layer_idx - 1])
            grad_low = grad_full.astype(jnp.bfloat16)
    return (grads, back_grad)


def body(
    dense_vec,
    q_tables,
    r_tables,
    owner,
    q_local,
    r_index,
    w_one,
    b_one,
    w_two,
    b_two,
    w_three,
    b_three,
    w_four,
    b_four,
    cotangent,
):
    layers = [(w_one, b_one), (w_two, b_two), (w_three, b_three), (w_four, b_four)]
    groups = lax.axis_size("group")
    batch_rows, table_count = q_local.shape
    embed_width = q_tables.shape[2]
    lookups = batch_rows * table_count
    capacity = 2 * lookups // groups
    slot_count = groups * capacity
    segment_count = q_tables.shape[0] * table_count
    table_ids = jnp.arange(table_count, dtype=jnp.int32)[None, :]
    highest = lax.Precision.HIGHEST
    dest_group = owner[:, :, 0]
    owner_hits = (
        dest_group[:, :, None] == jnp.arange(groups, dtype=jnp.int32)[None, None, :]
    ).astype(jnp.float32)
    table_lower = (jnp.arange(table_count)[:, None] < jnp.arange(table_count)[None, :]).astype(
        jnp.float32
    )
    sample_lower = (jnp.arange(batch_rows)[:, None] < jnp.arange(batch_rows)[None, :]).astype(
        jnp.float32
    )
    within = jnp.einsum("st,bsg->btg", table_lower, owner_hits, precision=highest)
    before = jnp.einsum("cb,cg->bg", sample_lower, jnp.sum(owner_hits, axis=1), precision=highest)
    slot_rank = jnp.sum((within + before[:, None, :]) * owner_hits, axis=2).astype(jnp.int32)
    position = (dest_group * capacity + slot_rank).reshape(lookups)
    source = (
        jnp.full((slot_count,), lookups, jnp.int32)
        .at[position]
        .set(jnp.arange(lookups, dtype=jnp.int32))
    )
    row_keys = (q_local * table_count + table_ids).reshape(lookups)
    keys_padded = jnp.concatenate([row_keys, jnp.zeros((1,), jnp.int32)])
    outgoing = keys_padded[source].reshape(groups, capacity)
    flat_table = q_tables.reshape(segment_count, embed_width)
    request = lax.all_to_all(outgoing, "group", split_axis=0, concat_axis=0, tiled=True)
    served_rows = flat_table[request].astype(jnp.bfloat16)
    arrived = lax.all_to_all(served_rows, "group", split_axis=0, concat_axis=0, tiled=True)
    q_rows = arrived.reshape(slot_count, embed_width)[position]
    full_r = lax.all_gather(r_tables, "local", axis=0, tiled=True)
    remainder_count = full_r.shape[0]
    r_pick = (
        r_index[:, :, None] == jnp.arange(remainder_count, dtype=jnp.int32)[None, None, :]
    ).astype(jnp.float32)
    r_rows = jnp.einsum("btr,rtd->btd", r_pick, full_r, precision=highest).reshape(
        lookups, embed_width
    )
    q_val = q_rows.astype(jnp.float32)
    embeds = (q_val * r_rows).astype(jnp.bfloat16).reshape(batch_rows, table_count, embed_width)
    vectors_all, features = interact(dense_vec, embeds)
    grads, d_features = dense_pass(features, layers, cotangent)
    d_embed = pair_back(d_features[:, embed_width:], vectors_all)[:, 1:, :].reshape(
        lookups, embed_width
    )
    grad_padded = jnp.concatenate(
        [d_embed * r_rows, jnp.zeros((1, embed_width), jnp.float32)], axis=0
    )
    outbound = grad_padded[source].reshape(groups, capacity, embed_width)
    returned = (
        lax.all_to_all(
            outbound.astype(jnp.bfloat16), "group", split_axis=0, concat_axis=0, tiled=True
        )
        .astype(outbound.dtype)
        .reshape(slot_count, embed_width)
    )
    served_flat = request.reshape(slot_count)
    q_part = jax.ops.segment_sum(returned, served_flat, num_segments=segment_count).reshape(
        q_tables.shape
    )
    q_piece = summed_on_arrival(q_part.astype(jnp.bfloat16), "local", 0)
    quarter = q_piece.shape[0]
    own_rows = lax.dynamic_slice_in_dim(q_tables, lax.axis_index("local") * quarter, quarter, 0)
    q_new = gather_directly(own_rows - table_rate * q_piece, "local", 0)
    r_part = jnp.einsum(
        "btr,btd->rtd",
        r_pick,
        (d_embed * q_val).reshape(batch_rows, table_count, embed_width),
        precision=highest,
    )
    summed = lax.psum(r_part, ("group", "local"))
    r_grad = lax.dynamic_slice_in_dim(
        summed, lax.axis_index("local") * r_tables.shape[0], r_tables.shape[0], 0
    )
    r_new = r_tables - table_rate * r_grad
    grad_wa, grad_ba, grad_wb, grad_bb, grad_wc, grad_bc, grad_wd, grad_bd = lax.psum(
        (
            grads[0][0],
            grads[0][1],
            grads[1][0],
            grads[1][1],
            grads[2][0],
            grads[2][1],
            grads[3][0],
            grads[3][1],
        ),
        ("group", "local"),
    )
    summed_grads = [(grad_wa, grad_ba), (grad_wb, grad_bb), (grad_wc, grad_bc), (grad_wd, grad_bd)]
    updated = []
    for (weight, biases), (w_grad, b_grad) in zip(layers, summed_grads):
        updated.append(weight.astype(jnp.float32) - dense_rate * w_grad)
        updated.append(biases - dense_rate * b_grad)
    return (
        q_new,
        r_new,
        updated[0],
        updated[1],
        updated[2],
        updated[3],
        updated[4],
        updated[5],
        updated[6],
        updated[7],
    )


def solution(mesh):
    return jax.shard_map(
        body,
        mesh=mesh,
        in_specs=(
            P(("group", "local"), None),
            P("group", None, None),
            P("local", None, None),
            P(("group", "local"), None, None),
            P(("group", "local"), None),
            P(("group", "local"), None),
            P(),
            P(),
            P(),
            P(),
            P(),
            P(),
            P(),
            P(),
            P(("group", "local"), None),
        ),
        out_specs=(
            P("group", None, None),
            P("local", None, None),
            P(),
            P(),
            P(),
            P(),
            P(),
            P(),
            P(),
            P(),
        ),
        check_vma=False,
    )
```

profile of v0, /device:TPU:1, one launch (start us, length us, event | category | flops | bytes accessed | tf_op | source)
XLA Modules:
  0.0 415.2 jit_solution(16516317859253861610)
XLA Ops:
  7.2 0.7 all-gather.2.cloned.1.call-update
  7.9 0.7 iota_add_fusion
  8.9 0.7 copy.131
  9.6 0.7 broadcast_multiply_fusion
  10.8 0.3 fusion.13
  11.4 12.8 %scatter_custom_fusion = s32[6656]{0:T(1024)S(1)} fusion(s32[3328]{0:T(1024)S(1)} %fusion.39, s32[3328]{0:T(1024)S(1)} %iota.29, s32[]{:T(128)} %constant.27.clone.1), kind=kCustom, calls=%fused_computation.86 | custom fusion | bytes 26628 | tf_op jit(solution)/shard_map/scatter | solution.py:145
  24.2 34.5 %gather_fusion = s32[6656]{0:T(1024)S(1)} fusion(s32[3329]{0:T(1024)S(1)} %pad_add_fusion, s32[7168]{0:T(1024)S(1)} %pad_clamp_fusion.1), kind=kCustom, calls=%fused_computation | custom fusion | bytes 79872 | tf_op jit(solution)/shard_map/gather | solution.py:149
  58.8 0.7 all_to_all.20
  59.5 9.6 %all-to-all-start = ((s32[32,1,208]{2,1,0:T(1,128)}), s32[32,1,208]{2,1,0:T(1,128)S(1)}, u32[]{:S(2)}, u32[]{:S(2)}) async-start(s32[32,1,208]{2,1,0:T(1,128)} %all_to_all.20), calls=%async_computation | async-start | bytes 65536 | tf_op jit(solution)/shard_map/all_to_all | solution.py:151
  69.1 2.5 copy.84
  71.8 4.6 %all-to-all-done = s32[32,1,208]{2,1,0:T(1,128)S(1)} async-done(((s32[32,1,208]{2,1,0:T(1,128)}), s32[32,1,208]{2,1,0:T(1,128)S(1)}, u32[]{:S(2)}, u32[]{:S(2)}) %all-to-all-start) | async-done | bytes 26656 | tf_op jit(solution)/shard_map/all_to_all | solution.py:151
  76.6 14.3 %gather_fusion.1 = bf16[6656,128]{1,0:T(8,128)(2,1)} fusion(bf16[3328,128]{1,0:T(8,128)(2,1)S(1)} %reshape.133, s32[7168]{0:T(1024)S(1)} %pad_clamp_fusion), kind=kCustom, calls=%fused_computation.1 | custom fusion | bytes 3434496 | tf_op jit(solution)/shard_map/gather | solution.py:152
  90.8 4.2 %all-to-all-start.1 = ((bf16[32,208,128]{2,1,0:T(8,128)(2,1)}), bf16[32,208,128]{2,1,0:T(8,128)(2,1)S(1)}, u32[]{:S(2)}, u32[]{:S(2)}) async-start(bf16[32,208,128]{2,1,0:T(8,128)(2,1)} %bitcast.56), calls=%async_computation.1 | async-start | bytes 3407872 | tf_op jit(solution)/shard_map/all_to_all | solution.py:153
  95.4 24.1 %all-to-all-done.1 = bf16[32,208,128]{2,1,0:T(8,128)(2,1)S(1)} async-done(((bf16[32,208,128]{2,1,0:T(8,128)(2,1)}), bf16[32,208,128]{2,1,0:T(8,128)(2,1)S(1)}, u32[]{:S(2)}, u32[]{:S(2)}) %all-to-all-start.1) | async-done | bytes 1703968 | tf_op jit(solution)/shard_map/all_to_all | solution.py:153
  119.5 6.5 %gather_fusion.2 = bf16[3328,128]{1,0:T(8,128)(2,1)S(1)} fusion(bf16[6656,128]{1,0:T(8,128)(2,1)S(1)} %bitcast.54, s32[4096]{0:T(1024)S(1)} %pad_clamp_fusion.2), kind=kCustom, calls=%fused_computation.2 | custom fusion | bytes 1717248 | tf_op jit(solution)/shard_map/gather | solution.py:154
  126.3 0.5 copy-done.15
  126.8 7.3 %fusion.5 = (bf16[128,26,128]{2,0,1:T(8,128)(2,1)S(1)}, f32[26,128,128]{2,1,0:T(8,128)}) fusion(f32[128,26,128]{2,1,0:T(8,128)S(1)} %reshape.138, f32[256,26,128]{2,0,1:T(8,128)} %all-gather.2.cloned.1.call-done, s32[128,26]{0,1:T(8,128)S(1)} %copy-done.15), kind=kOutput, calls=%fused_computation.19 | convolution fusion | flops 1310326784 | bytes 7681024 | tf_op jit(solution)/shard_map/btr,rtd->btd/dot_general | solution.py:160
  134.1 0.7 fusion.16
  134.8 1.1 copy.92
  135.9 4.9 %gather_fusion.3 = bf16[351,128]{1,0:T(8,128)(2,1)S(1)} fusion(bf16[128,27,27]{0,2,1:T(8,128)(2,1)S(1)} %copy.92, s32[351]{0:T(512)S(1)} %copy-done), kind=kCustom, calls=%fused_computation.3 | custom fusion | bytes 182520 | tf_op jit(solution)/shard_map/gather | solution.py:48
  140.8 1.5 convolution_add_fusion
  142.4 2.1 convolution_add_fusion.2
  144.6 0.4 convolution_add_fusion.3
  145.0 0.6 copy-done.12
  145.8 0.5 fusion.44
  146.3 1.1 copy-done.7
  147.4 0.9 fusion.43
  148.2 0.3 copy-done.5
  148.6 0.3 convolution_bitcast_fusion
  148.9 1.7 fusion.23
  150.6 2.8 fusion.26
  153.4 1.8 fusion.30
  155.2 1.1 fusion.22
  156.3 19.0 %scatter_fusion = f32[128,27,27]{0,2,1:T(8,128)S(1)} fusion(f32[128,27,27]{0,2,1:T(8,128)S(1)} %broadcast_in_dim.23, s32[351]{0:T(512)S(1)} %copy-done, f32[351,128]{1,0:T(8,128)S(1)} %convolution_bitcast_fusion), kind=kCustom, calls=%fused_computation.6 | custom fusion | bytes 541944 | tf_op jit(solution)/shard_map/scatter | solution.py:61
  175.6 2.9 copy.111
  178.5 3.3 fusion.14
  181.9 6.2 %fusion.4 = f32[256,26,128]{0,2,1:T(8,128)} fusion(s32[128,26]{0,1:T(8,128)S(1)} %copy-done.15, f32[128,26,128]{2,1,0:T(8,128)S(1)} %fusion.14, f32[128,26,128]{2,1,0:T(8,128)S(1)} %copy-done.2), kind=kOutput, calls=%fused_computation.16 | convolution fusion | flops 1309900800 | bytes 6829056 | tf_op jit(solution)/shard_map/btr,btd->rtd/dot_general | solution.py:189
  188.1 2.5 bitcast_multiply_fusion
  190.6 0.6 copy.98
  191.5 14.3 %gather_fusion.4 = bf16[6656,128]{1,0:T(8,128)(2,1)} fusion(bf16[3329,128]{1,0:T(8,128)(2,1)S(1)} %concatenate.24, s32[7168]{0:T(1024)S(1)} %pad_clamp_fusion.1), kind=kCustom, calls=%fused_computation.4 | custom fusion | bytes 3434496 | tf_op jit(solution)/shard_map/gather | solution.py:173
  205.8 5.0 %all-to-all-start.2 = ((bf16[32,208,128]{2,1,0:T(8,128)(2,1)}), bf16[32,208,128]{2,1,0:T(8,128)(2,1)S(1)}, u32[]{:S(2)}, u32[]{:S(2)}) async-start(bf16[32,208,128]{2,1,0:T(8,128)(2,1)} %bitcast.10), calls=%async_computation.2 | async-start | bytes 3407872 | tf_op jit(solution)/shard_map/all_to_all | solution.py:175
  210.9 28.2 %all-to-all-done.2 = bf16[32,208,128]{2,1,0:T(8,128)(2,1)S(1)} async-done(((bf16[32,208,128]{2,1,0:T(8,128)(2,1)}), bf16[32,208,128]{2,1,0:T(8,128)(2,1)S(1)}, u32[]{:S(2)}, u32[]{:S(2)}) %all-to-all-start.2) | async-done | bytes 1703968 | tf_op jit(solution)/shard_map/all_to_all | solution.py:175
  239.2 42.1 %scatter_custom_fusion.2 = f32[3328,128]{1,0:T(8,128)S(1)} fusion(s32[6656]{0:T(1024)S(1)} %reshape.195, bf16[6656,128]{1,0:T(8,128)(2,1)S(1)} %bitcast.55, f32[]{:T(128)} %constant.24.clone.1), kind=kCustom, calls=%fused_computation.9 | custom fusion | flops 1703936 | bytes 3407876 | tf_op jit(solution)/shard_map/scatter-add | solution.py:182
  281.3 1.0 convert_element_type.102
  282.3 1.3 convert_element_type.103
  283.6 1.2 copy.99
  284.8 3.9 all-to-all-start.3
  288.7 8.7 %all-to-all-done.3 = bf16[4,32,26,128]{3,1,2,0:T(8,128)(2,1)S(1)} async-done(((bf16[4,32,26,128]{3,1,2,0:T(8,128)(2,1)}), bf16[4,32,26,128]{3,1,2,0:T(8,128)(2,1)S(1)}, u32[]{:S(2)}, u32[]{:S(2)}) %all-to-all-start.3) | async-done | bytes 852000 | tf_op jit(solution)/shard_map/all_to_all | solution.py:18
  297.5 1.3 fusion.20
  298.8 0.3 copy.101
  299.1 1.4 broadcast_in_dim.29
  300.5 3.6 all-to-all-start.4
  304.1 1.7 copy.105
  305.8 85.5 %all-reduce.1 = (f32[1024]{0:T(1024)S(1)}, f32[1024]{0:T(1024)S(1)}, f32[512]{0:T(512)S(1)}, f32[256]{0:T(256)S(1)}) all-reduce(f32[1024]{0:T(1024)S(1)} %get-tuple-element.61, f32[1024]{0:T(1024)S(1)} %get-tuple-element.63, f32[512]{0:T(512)S(1)} %get-tuple-element.65, ...), channel_id=1, replica_groups=mesh['group'=32,'local'=4] {'group','local'}, use_global_device_ids=true, to_apply=%region_9.10 | all-reduce | flops 2816 | bytes 22528 | tf_op jit(solution)/shard_map/psum | solution.py:200
  391.3 0.6 multiply_subtract_fusion.8
  391.9 0.6 multiply_subtract_fusion.7
  392.5 0.6 multiply_subtract_fusion.5
  393.1 1.4 copy.102
  394.5 2.0 multiply_subtract_fusion.3
  396.4 1.4 copy.106
  397.8 3.4 multiply_subtract_fusion.2
  401.3 4.5 %multiply_subtract_fusion = f32[1024,1024]{1,0:T(8,128)} fusion(f32[1024,1024]{1,0:T(8,128)S(1)} %copy-done.4, bf16[1024,1024]{1,0:T(8,128)(2,1)} %param.31), kind=kLoop, calls=%fused_computation.8 | loop fusion | flops 3145728 | bytes 10485760 | tf_op jit(solution)/shard_map/sub | solution.py:216
  405.8 1.7 multiply_subtract_fusion.1
  407.5 0.9 multiply_subtract_fusion.4
  (76 shorter events, 3.4 us)
Async XLA Ops:
  7.2 119.1 %all-gather.2.cloned.1.call-start = ((), (), s32[]{:S(2)}) async-start(), calls=%async_computation.5 | async-start | bytes 4259840 | tf_op jit(solution)/shard_map/all_gather | solution.py:155
  59.5 16.9 %all-to-all-start = ((s32[32,1,208]{2,1,0:T(1,128)}), s32[32,1,208]{2,1,0:T(1,128)S(1)}, u32[]{:S(2)}, u32[]{:S(2)}) async-start(s32[32,1,208]{2,1,0:T(1,128)} %all_to_all.20), calls=%async_computation | async-start | bytes 65536 | tf_op jit(solution)/shard_map/all_to_all | solution.py:151
  71.6 19.3 %copy-start.3 = (f32[128,26,128]{2,1,0:T(8,128)}, f32[128,26,128]{2,1,0:T(8,128)S(1)}, u32[]{:S(2)}) copy-start(f32[128,26,128]{2,1,0:T(8,128)S(1)} %copy.84) | copy-start | bytes 5111812
  90.8 4.4 %copy-start.14 = (bf16[128,128]{1,0:T(8,128)(2,1)S(1)}, bf16[128,128]{1,0:T(8,128)(2,1)}, u32[]{:S(2)}) copy-start(bf16[128,128]{1,0:T(8,128)(2,1)} %param.23) | copy-start | bytes 98308
  90.8 28.7 %all-to-all-start.1 = ((bf16[32,208,128]{2,1,0:T(8,128)(2,1)}), bf16[32,208,128]{2,1,0:T(8,128)(2,1)S(1)}, u32[]{:S(2)}, u32[]{:S(2)}) async-start(bf16[32,208,128]{2,1,0:T(8,128)(2,1)} %bitcast.56), calls=%async_computation.1 | async-start | bytes 3407872 | tf_op jit(solution)/shard_map/all_to_all | solution.py:153
  95.0 299.5 %all-reduce.5.cloned.1.call-start = ((), (), s32[]{:S(2)}) async-start(), calls=%async_computation.6 | async-start | bytes 24379392 | tf_op jit(solution)/shard_map/psum | solution.py:195
  126.0 0.7 copy-start.15
  126.2 7.8 %copy-start.1 = (f32[128,26,128]{2,1,0:T(8,128)}, f32[128,26,128]{2,1,0:T(8,128)S(1)}, u32[]{:S(2)}) copy-start(f32[128,26,128]{2,1,0:T(8,128)S(1)} %reshape.138) | copy-start | bytes 5111812
  134.1 1.8 copy-start
  134.1 6.7 %copy-start.17 = (f32[1024]{0:T(1024)S(1)}, f32[1024]{0:T(1024)}, u32[]{:S(2)}) copy-start(f32[1024]{0:T(1024)} %param.30) | copy-start | bytes 12292
  134.8 7.6 %copy-start.18 = (f32[1024]{0:T(1024)S(1)}, f32[1024]{0:T(1024)}, u32[]{:S(2)}) copy-start(f32[1024]{0:T(1024)} %param.32) | copy-start | bytes 12292
  142.4 2.2 copy-start.9
  142.4 2.2 copy-start.19
  144.6 1.0 copy-start.12
  144.6 0.9 copy-start.16
  145.8 1.6 copy-start.7
  147.4 1.2 copy-start.5
  178.5 3.4 copy-start.2
  205.8 33.4 %all-to-all-start.2 = ((bf16[32,208,128]{2,1,0:T(8,128)(2,1)}), bf16[32,208,128]{2,1,0:T(8,128)(2,1)S(1)}, u32[]{:S(2)}, u32[]{:S(2)}) async-start(bf16[32,208,128]{2,1,0:T(8,128)(2,1)} %bitcast.10), calls=%async_computation.2 | async-start | bytes 3407872 | tf_op jit(solution)/shard_map/all_to_all | solution.py:175
  284.8 12.6 %all-to-all-start.3 = ((bf16[4,32,26,128]{3,1,2,0:T(8,128)(2,1)}), bf16[4,32,26,128]{3,1,2,0:T(8,128)(2,1)S(1)}, u32[]{:S(2)}, u32[]{:S(2)}) async-start(bf16[4,32,26,128]{3,1,2,0:T(8,128)(2,1)} %copy.99), calls=%async_computation.3 | async-start | bytes 1703936 | tf_op jit(solution)/shard_map/all_to_all | solution.py:18
  300.5 92.6 %all-to-all-start.4 = ((f32[4,32,26,128]{3,1,2,0:T(8,128)}), f32[4,32,26,128]{3,1,2,0:T(8,128)S(1)}, u32[]{:S(2)}, u32[]{:S(2)}) async-start(f32[4,32,26,128]{3,1,2,0:T(8,128)} %broadcast_in_dim.29), calls=%async_computation.4 | async-start | bytes 3407872 | tf_op jit(solution)/shard_map/all_to_all | solution.py:30
  304.1 87.3 %copy-start.20 = (f32[256]{0:T(256)S(1)}, f32[256]{0:T(256)}, u32[]{:S(2)}) copy-start(f32[256]{0:T(256)} %param.36) | copy-start | bytes 3076
  396.4 1.4 copy-start.6
  397.8 3.4 copy-start.4
  401.3 4.5 %copy-start.8 = (f32[1024,512]{1,0:T(8,128)S(1)}, f32[1024,512]{1,0:T(8,128)}, u32[]{:S(2)}) copy-start(f32[1024,512]{1,0:T(8,128)} %get-tuple-element.57) | copy-start | bytes 6291460
  401.3 4.5 %copy-start.10 = (bf16[1024,512]{1,0:T(8,128)(2,1)S(1)}, bf16[1024,512]{1,0:T(8,128)(2,1)}, u32[]{:S(2)}) copy-start(bf16[1024,512]{1,0:T(8,128)(2,1)} %param.33) | copy-start | bytes 3145732
  405.8 1.7 copy-start.11
  405.8 1.7 copy-start.13
Sparse Core Ops, SparseCore 0:
  9.6 44.6 all-gather.1
  188.2 188.7 all-reduce.4
where the time goes:
time: 415 us
  local copies, waits for them, and re-layouts  128 us (31%)
  blocking collectives  85.5 us (21%)
  waiting for transfers between devices  66.3 us (16%)
  other arithmetic  63.4 us (15%)
  matrix products  31.2 us (8%)
  starting transfers between devices  26.5 us (6%)
  between operations  14.6 us (4%)
    psum x1, blocking collectives, body(): lax.psum((grads[0][0], grads[0][1], grads[1][0], grads[1][1], grads[2][0]...  85.5 us
    scatter-add x1, other arithmetic, body(): jax.ops.segment_sum(returned, served_flat, num_segments=segment_count)  42.1 us
    gather x1, local copies, waits for them, and re-layouts, body(): outgoing = keys_padded[source].reshape(groups, capacity)  34.5 us
    all_to_all x1, waiting for transfers between devices, body(): lax.all_to_all(outbound.astype(jnp.bfloat16), 'group', split_axis=0, conc...  28.2 us
    all_to_all x1, waiting for transfers between devices, body(): lax.all_to_all(served_rows, 'group', split_axis=0, concat_axis=0, tiled=T...  24.1 us
    scatter x1, local copies, waits for them, and re-layouts, pair_back(): spread = jnp.zeros((vectors_all.shape[0], vectors, vectors), jnp.float32)...  19 us
    gather x1, local copies, waits for them, and re-layouts, body(): served_rows = flat_table[request].astype(jnp.bfloat16)  14.3 us
    gather x1, local copies, waits for them, and re-layouts, body(): outbound = grad_padded[source].reshape(groups, capacity, embed_width)  14.3 us
  transfers between devices with their start and end apart: 7, of which 4 were waited for; matrix products, arithmetic and copies ran while one was open for 35% of the time, Pallas kernels for 0%

commit v1 on v0

v1 whole, which is shorter than its diff:
```python
import jax
import jax.numpy as jnp
import numpy as np
from jax import lax
from jax.experimental import pallas as pl
from jax.experimental.pallas import tpu as pltpu
from jax.sharding import PartitionSpec as P

table_rate = 0.05
dense_rate = 0.0005
BF = jnp.bfloat16
F32 = jnp.float32
I32 = jnp.int32

GROUPS = 32
LOCALS = 4
TABLES = 26
ROWS = 128
DIM = 128
CAP = 208
LOOKUPS = TABLES * ROWS
SLOTS = GROUPS * CAP
FEAT = 479
PAIRS = 351
REM = 256
BOTH = ("group", "local")
CORE_PAIRS = [[2 * i, 2 * i + 1] for i in range(GROUPS // 2)]
SAME_CORE = [list(range(c, GROUPS, 2)) for c in range(2)]
SAME_CORE_ALL = [
    [g * LOCALS + l for g in range(c, GROUPS, 2) for l in range(LOCALS)] for c in range(2)
]
VMEM_LIMIT = 20 * 1024 * 1024


def smem():
    return pl.BlockSpec(memory_space=pltpu.SMEM)


def vmem():
    return pl.BlockSpec(memory_space=pltpu.VMEM)


def call(kernel, out, in_specs, scratch, name):
    return pl.pallas_call(
        kernel,
        out_shape=out,
        in_specs=in_specs,
        out_specs=vmem(),
        scratch_shapes=scratch,
        compiler_params=pltpu.CompilerParams(vmem_limit_bytes=VMEM_LIMIT),
        name=name,
    )


def serve_kernel(keys, table, out, rows):
    def step(g, carry):
        for c in range(CAP):
            rows[c : c + 1, :] = table[pl.ds(keys[g, c], 1), :]
        out[g] = rows[...].astype(BF)
        return carry

    lax.fori_loop(0, GROUPS, step, 0)


def serve(keys, table):
    return call(
        serve_kernel,
        jax.ShapeDtypeStruct((GROUPS, CAP, DIM), BF),
        [smem(), vmem()],
        [pltpu.VMEM((CAP, DIM), F32)],
        "serve_rows",
    )(keys, table)


ALL_PAIRS = 384
IDS = 32
BLOCK = 256
NEXT = 28 * IDS


def sigma_of(preact):
    sigma = jax.nn.sigmoid(preact)
    return (preact * sigma).astype(BF), sigma * (1.0 + preact * (1.0 - sigma))


def times(left, right):
    return jnp.dot(left, right, preferred_element_type=F32)


def times_turned(left, right):
    return lax.dot_general(left, right, (((1,), (1,)), ((), ())), preferred_element_type=F32)


def every(first):
    return pl.ds(first, ROWS, stride=IDS)


def compute_kernel(
    position,
    arrived,
    r_rows,
    dense,
    w_one,
    b_one,
    w_two,
    b_two,
    w_three,
    b_three,
    w_four,
    cot,
    select,
    mirror,
    outbound,
    feats,
    act_one,
    act_two,
    act_three,
    grad_one,
    grad_two,
    grad_three,
    d_low,
    sums,
    wide,
    rows,
    q_rows,
    tall,
    low,
    mixed,
):
    def group_rows(g):
        return pl.ds(pl.multiple_of(g * CAP, 16), CAP)

    def widen(g, carry):
        wide[group_rows(g), :] = arrived[g].astype(F32)
        return carry

    lax.fori_loop(0, GROUPS, widen, 0)
    tall[every(0), :] = dense[...].astype(F32)
    for i in range(TABLES + 1, IDS):
        tall[every(i), :] = jnp.zeros((ROWS, DIM), F32)

    def embed(t, carry):
        for b in range(ROWS):
            rows[b : b + 1, :] = wide[pl.ds(position[t, b], 1), :]
        values = rows[...]
        q_rows[t] = values
        tall[every(t + 1), :] = (values * r_rows[t]).astype(BF).astype(F32)
        return carry

    lax.fori_loop(0, TABLES, embed, 0)

    row_id = lax.broadcasted_iota(I32, (BLOCK, BLOCK), 0)
    lane_id = lax.broadcasted_iota(I32, (BLOCK, BLOCK), 1)
    same = (row_id // IDS) == (lane_id // IDS)
    row_id = lax.broadcasted_iota(I32, (BLOCK, DIM), 0)
    lane_id = lax.broadcasted_iota(I32, (BLOCK, DIM), 1)
    fold = ((row_id % IDS) == (lane_id % IDS)).astype(BF)
    quarter = (row_id % 4) == (lane_id // IDS)

    def block(n):
        return pl.ds(pl.multiple_of(n * BLOCK, BLOCK), BLOCK)

    def gram(n, carry):
        own = tall[block(n), :].astype(BF)
        low[block(n), :] = own
        products = jnp.where(same, times_turned(own, own), 0.0).astype(BF)
        mixed[block(n), :] = jnp.where(quarter, times(products, fold), 0.0)
        return carry

    lax.fori_loop(0, ROWS * IDS // BLOCK, gram, 0)
    grams = []
    for m in range(7):
        part = mixed[every(4 * m), :]
        for k in range(1, 4):
            part = part + mixed[every(4 * m + k), :]
        grams.append(part.astype(BF))
    pairs = times(jnp.concatenate(grams, axis=1), select[...])
    lane = lax.broadcasted_iota(I32, (ROWS, ALL_PAIRS), 1)
    pairs = jnp.where(lane == PAIRS, 1.0, pairs)
    feats[:, :DIM] = dense[...]
    feats[:, DIM:] = pairs.astype(BF)

    act, slope_one = sigma_of(times(feats[...], w_one[...]) + b_one[...])
    act_one[...] = act
    act, slope_two = sigma_of(times(act, w_two[...]) + b_two[...])
    act_two[...] = act
    act, slope_three = sigma_of(times(act, w_three[...]) + b_three[...])
    act_three[...] = act

    full = times_turned(cot[...], w_four[...]) * slope_three
    sums[...] = jnp.zeros((8, 1024), F32)
    sums[1:2, :512] = jnp.sum(full, axis=0, keepdims=True)
    sums[1:2, 512:768] = jnp.sum(cot[...].astype(F32), axis=0, keepdims=True)
    grad = full.astype(BF)
    grad_three[...] = grad
    full = times_turned(grad, w_three[...]) * slope_two
    sums[0:1, :] = jnp.sum(full, axis=0, keepdims=True)
    grad = full.astype(BF)
    grad_two[...] = grad
    grad = (times_turned(grad, w_two[...]) * slope_one).astype(BF)
    grad_one[...] = grad
    d_pairs = times_turned(grad, w_one[DIM:, :])
    high = d_pairs.astype(BF)
    spread = times(high, mirror[...])
    lane = lax.broadcasted_iota(I32, (ROWS, DIM), 1) // IDS
    for m in range(7):
        part = spread[:, m * DIM : (m + 1) * DIM]
        for k in range(4):
            mixed[every(4 * m + k), :] = jnp.where(lane == k, part, 0.0)

    def back(n, carry):
        unfolded = times_turned(mixed[block(n), :].astype(BF), fold)
        unfolded = jnp.where(same, unfolded, 0.0).astype(BF)
        tall[block(n), :] = times(unfolded, low[block(n), :])
        return carry

    lax.fori_loop(0, ROWS * IDS // BLOCK, back, 0)

    def clear(g, carry):
        wide[group_rows(g), :] = jnp.zeros((CAP, DIM), F32)
        return carry

    lax.fori_loop(0, GROUPS, clear, 0)

    def route(t, carry):
        d_embed = tall[every(t + 1), :]
        d_low[t] = (d_embed * q_rows[t]).astype(BF)
        rows[...] = d_embed * r_rows[t]
        for b in range(ROWS):
            wide[pl.ds(position[t, b], 1), :] = rows[b : b + 1, :]
        return carry

    lax.fori_loop(0, TABLES, route, 0)

    def narrow(g, carry):
        outbound[g] = wide[group_rows(g), :].astype(BF)
        return carry

    lax.fori_loop(0, GROUPS, narrow, 0)


def compute(position, *arrays):
    shape = jax.ShapeDtypeStruct
    return pl.pallas_call(
        compute_kernel,
        out_shape=(
            shape((GROUPS, CAP, DIM), BF),
            shape((ROWS, DIM + ALL_PAIRS), BF),
            shape((ROWS, 1024), BF),
            shape((ROWS, 1024), BF),
            shape((ROWS, 512), BF),
            shape((ROWS, 1024), BF),
            shape((ROWS, 1024), BF),
            shape((ROWS, 512), BF),
            shape((TABLES, ROWS, DIM), BF),
            shape((8, 1024), F32),
        ),
        in_specs=[smem()] + [vmem()] * len(arrays),
        out_specs=(vmem(),) * 10,
        scratch_shapes=[
            pltpu.VMEM((SLOTS, DIM), F32),
            pltpu.VMEM((ROWS, DIM), F32),
            pltpu.VMEM((TABLES, ROWS, DIM), F32),
            pltpu.VMEM((ROWS * IDS, DIM), F32),
            pltpu.VMEM((ROWS * IDS, DIM), BF),
            pltpu.VMEM((ROWS * IDS, DIM), F32),
        ],
        compiler_params=pltpu.CompilerParams(vmem_limit_bytes=40 * 1024 * 1024),
        name="compute_step",
    )(position, *arrays)


DENSE_LANES = 2176
R_LANES = 7 * DIM
PACKED = DENSE_LANES + R_LANES
HALF_TABLES = 14


def weight_kernel(
    feats, act_one, act_two, act_three, grad_one, grad_two, grad_three, cot, d_low, r_row, sums, out
):
    def contract(left, first, right):
        return lax.dot_general(
            left[:, first : first + BLOCK],
            right,
            (((0,), (0,)), ((), ())),
            preferred_element_type=F32,
        ).astype(BF)

    for first in range(0, 1024, BLOCK):
        out[first : first + BLOCK, :1024] = contract(act_one, first, grad_two[...])
        out[first : first + BLOCK, 1024:1536] = contract(act_two, first, grad_three[...])
    for first in range(0, 512, BLOCK):
        for half in range(2):
            out[half * 512 + first : half * 512 + first + BLOCK, 1536:2048] = contract(
                feats, first, grad_one[:, half * 512 : half * 512 + 512]
            )
            out[half * 512 + first : half * 512 + first + BLOCK, 2048:2176] = contract(
                act_three, first, cot[:, half * DIM : half * DIM + DIM]
            )
    row = lax.broadcasted_iota(I32, (32, 512), 0)
    for half in range(2):
        at = slice(half * 512, half * 512 + 512)
        tail = jnp.where(
            row == 0, sums[0:1, at], jnp.where(row == 1, sums[1:2, at], jnp.zeros((32, 512), F32))
        )
        out[half * 512 + 480 : half * 512 + 512, 1536:2048] = tail.astype(BF)

    rem = lax.broadcasted_iota(I32, (REM, ROWS), 0)
    for t in range(2 * HALF_TABLES):
        core, within = divmod(t, HALF_TABLES)
        if t < TABLES:
            pick = (rem == r_row[t]).astype(BF)
            part = times(pick, d_low[t]).astype(BF)
        else:
            part = jnp.zeros((REM, DIM), BF)
        for l in range(LOCALS):
            for j in range(8):
                zy, k = divmod(within * 8 + j, 7)
                top = core * 512 + (zy * LOCALS + l) * 8
                left = DENSE_LANES + k * DIM
                first = l * 64 + j * 8
                out[top : top + 8, left : left + DIM] = part[first : first + 8, :]


def weight_grads(*arrays):
    return call(
        weight_kernel,
        jax.ShapeDtypeStruct((1024, PACKED), BF),
        [vmem()] * len(arrays),
        [],
        "weight_grads",
    )(*arrays)


LANES = 4
CHUNK = 16


def segment_kernel(keys, returned, out, wide, *sums):
    def widen(g, carry):
        wide[pl.ds(pl.multiple_of(g * CAP, 16), CAP), :] = returned[g].astype(F32)
        return carry

    lax.fori_loop(0, GROUPS, widen, 0)

    def clear(t, carry):
        at = pl.ds(pl.multiple_of(t * ROWS, 16), ROWS)
        for part in sums:
            part[at, :] = jnp.zeros((ROWS, DIM), F32)
        return carry

    lax.fori_loop(0, TABLES, clear, 0)
    share = GROUPS // LANES

    def step(i, carry):
        inner = i // (CAP // CHUNK)
        first = pl.multiple_of((i % (CAP // CHUNK)) * CHUNK, CHUNK)
        for c in range(CHUNK):
            for k in range(LANES):
                g = k * share + inner
                at = pl.ds(keys[g, first + c], 1)
                sums[k][at, :] = sums[k][at, :] + wide[pl.ds(g * CAP + first + c, 1), :]
        return carry

    lax.fori_loop(0, share * (CAP // CHUNK), step, 0)

    def finish(t, carry):
        at = pl.ds(pl.multiple_of(t * ROWS, 16), ROWS)
        total = sums[0][at, :]
        for part in sums[1:]:
            total = total + part[at, :]
        out[at, :] = total.astype(BF)
        return carry

    lax.fori_loop(0, TABLES, finish, 0)


def segment_rows(keys, returned):
    return call(
        segment_kernel,
        jax.ShapeDtypeStruct((LOOKUPS, DIM), BF),
        [smem(), vmem()],
        [pltpu.VMEM((SLOTS, DIM), F32)] + [pltpu.VMEM((LOOKUPS, DIM), F32)] * LANES,
        "segment_rows",
    )(keys, returned)


def pair_columns():
    vectors = TABLES + 1
    lower = np.full((28, IDS), -1, np.int32)
    lower_i, lower_j = np.tril_indices(vectors, -1)
    lower[lower_i, lower_j] = np.arange(PAIRS)
    both = lower.copy()
    both[lower_j, lower_i] = np.arange(PAIRS)
    return (lower.reshape(NEXT), both.reshape(NEXT))


def summed(blocks):
    return blocks.astype(F32).sum(axis=0).astype(BF)


def pair_summed(blocks):
    return summed(
        lax.all_to_all(blocks, "group", 0, 0, tiled=True, axis_index_groups=CORE_PAIRS)
    )


def pair_gathered(block):
    return lax.all_to_all(
        jnp.broadcast_to(block[None], (2, *block.shape)),
        "group",
        0,
        0,
        tiled=True,
        axis_index_groups=CORE_PAIRS,
    )


def body(
    dense_vec,
    q_tables,
    r_tables,
    owner,
    q_local,
    r_index,
    w_one,
    b_one,
    w_two,
    b_two,
    w_three,
    b_three,
    w_four,
    b_four,
    cotangent,
):
    dest = owner[:, :, 0].T
    q_row = q_local.T
    r_row = r_index.T
    hits = (dest[:, :, None] == jnp.arange(GROUPS, dtype=I32)).astype(BF)
    earlier = (jnp.arange(ROWS)[:, None] > jnp.arange(ROWS)[None, :]).astype(BF)
    within = jnp.einsum("cb,tbg->tcg", earlier, hits, preferred_element_type=F32)
    counts = jnp.sum(hits.astype(F32), axis=1)
    tables_before = (jnp.arange(TABLES)[:, None] > jnp.arange(TABLES)[None, :]).astype(F32)
    before = jnp.dot(tables_before, counts, precision=lax.Precision.HIGHEST)
    rank = jnp.sum((within + before[:, None, :]) * hits.astype(F32), axis=2).astype(I32)
    position = dest * CAP + rank
    ranks = (rank[:, :, None] == jnp.arange(CAP, dtype=I32)).astype(BF)
    table_ids = jnp.arange(TABLES, dtype=I32)[:, None, None].astype(BF)
    tagged = jnp.concatenate([hits * q_row[:, :, None].astype(BF), hits * table_ids], axis=2)
    slots = jnp.einsum("tbg,tbc->gc", tagged, ranks, preferred_element_type=F32).astype(I32)
    outgoing = slots[GROUPS:] * ROWS + slots[:GROUPS]

    request = lax.all_to_all(outgoing, "group", 0, 0, tiled=True)
    table_rows = jnp.swapaxes(q_tables, 0, 1).reshape(LOOKUPS, DIM)
    served = serve(request, table_rows)
    arrived = lax.all_to_all(served, "group", 0, 0, tiled=True)

    full_r = lax.all_gather(r_tables, "local", axis=0, tiled=True)
    r_pick = (r_row[:, :, None] == jnp.arange(REM, dtype=I32)).astype(BF)
    r_high = lax.reduce_precision(full_r, 8, 7)
    r_low = full_r - r_high
    r_rows = jnp.einsum(
        "tbr,rtd->tbd", r_pick, r_high.astype(BF), preferred_element_type=F32
    ) + jnp.einsum("tbr,rtd->tbd", r_pick, r_low.astype(BF), preferred_element_type=F32)

    lower, both = pair_columns()
    columns = jnp.arange(ALL_PAIRS, dtype=I32)
    select = (jnp.asarray(lower)[:, None] == columns[None, :]).astype(BF)
    mirror = (jnp.asarray(both)[None, :] == columns[:, None]).astype(BF)
    w_padded = jnp.pad(w_one, ((0, 33), (0, 0)))
    arrived, r_rows, select, mirror, w_padded, table_rows = lax.optimization_barrier(
        (arrived, r_rows, select, mirror, w_padded, table_rows)
    )
    outbound, *saved, d_low, sums = compute(
        position,
        arrived,
        r_rows,
        dense_vec,
        w_padded,
        b_one[None],
        w_two,
        b_two[None],
        w_three,
        b_three[None],
        w_four,
        cotangent,
        select,
        mirror,
    )
    returned = lax.all_to_all(outbound, "group", 0, 0, tiled=True)

    packed = weight_grads(*saved, cotangent, d_low, r_row[:, None, :], sums)
    half = pair_summed(packed.reshape(2, 512, PACKED)).reshape(2 * GROUPS, 8, PACKED)
    own = summed(
        lax.all_to_all(half, BOTH, 0, 0, tiled=True, axis_index_groups=SAME_CORE_ALL)
    )
    w_half = lax.all_to_all(
        jnp.broadcast_to(own[None, :, :DENSE_LANES], (2 * GROUPS, 8, DENSE_LANES)),
        BOTH,
        0,
        0,
        tiled=True,
        axis_index_groups=SAME_CORE_ALL,
    ).reshape(512, DENSE_LANES)
    w_all = pair_gathered(w_half).reshape(1024, DENSE_LANES)
    r_half = lax.all_to_all(
        jnp.broadcast_to(own[None, :, DENSE_LANES:], (GROUPS // 2, 8, R_LANES)),
        "group",
        0,
        0,
        tiled=True,
        axis_index_groups=SAME_CORE,
    )
    r_grad = pair_gathered(r_half).reshape(2, GROUPS // 2, 8, 7, DIM)
    r_grad = jnp.swapaxes(r_grad, 2, 3).reshape(28, 64, DIM)[:TABLES]
    r_new = r_tables - table_rate * jnp.swapaxes(r_grad, 0, 1).astype(F32)

    q_part = segment_rows(request, returned)
    q_piece = summed(
        lax.all_to_all(q_part.reshape(LOCALS, LOOKUPS // LOCALS, DIM), "local", 0, 0, tiled=True)
    )
    q_grad = lax.all_gather(q_piece, "local", axis=0, tiled=True).reshape(TABLES, ROWS, DIM)
    q_new = q_tables - table_rate * jnp.swapaxes(q_grad, 0, 1).astype(F32)

    first = w_all[:, 1536:2048]
    first = jnp.concatenate([first[:512], first[512:]], axis=1).astype(F32)
    last = w_all[:, 2048:]
    last = jnp.concatenate([last[:512], last[512:]], axis=1).astype(F32)
    return (
        q_new,
        r_new,
        w_one.astype(F32) - dense_rate * first[:FEAT],
        b_one - dense_rate * first[FEAT],
        w_two.astype(F32) - dense_rate * w_all[:, :1024].astype(F32),
        b_two - dense_rate * first[FEAT + 1],
        w_three.astype(F32) - dense_rate * w_all[:, 1024:1536].astype(F32),
        b_three - dense_rate * first[FEAT + 2, :512],
        w_four.astype(F32) - dense_rate * last,
        b_four - dense_rate * first[FEAT + 2, 512:768],
    )


def solution(mesh):
    rows = P(("group", "local"), None)
    return jax.shard_map(
        body,
        mesh=mesh,
        in_specs=(
            rows,
            P("group", None, None),
            P("local", None, None),
            P(("group", "local"), None, None),
            rows,
            rows,
            P(),
            P(),
            P(),
            P(),
            P(),
            P(),
            P(),
            P(),
            rows,
        ),
        out_specs=(
            P("group", None, None),
            P("local", None, None),
            P(),
            P(),
            P(),
            P(),
            P(),
            P(),
            P(),
            P(),
        ),
        check_vma=False,
    )
```

time: 415 us -> 303 us (0.73)
  local copies, waits for them, and re-layouts: 128 us -> 11.4 us
  Pallas kernels: 0 us -> 56.2 us
  other arithmetic: 63.4 us -> 24.3 us
  matrix products: 31.2 us -> 5.69 us
  waiting for transfers between devices: 66.3 us -> 79.6 us
  blocking collectives: 85.5 us -> 79 us
  starting transfers between devices: 26.5 us -> 30.8 us
    psum x1 -> x0, blocking collectives: 85.5 us -> none  [body(): lax.psum((grads[0][0], grads[0][1], grads[1][0], grads[1][1], grads[2][0]...]
    gather x5 -> x0, local copies, waits for them, and re-layouts: 74.5 us -> none  [the longest x1 34.5 us: body(): outgoing = keys_padded[source].reshape(groups, capacity)]
    pallas_call x0 -> x4, Pallas kernels: none -> 56.2 us  [the longest x1 27.2 us: compute(): pl.pallas_call(compute_kernel, out_shape=(shape((GROUPS, CAP, DIM), BF),...]
    all_to_all x0 -> x4, blocking collectives: none -> 45.2 us  [the longest x2 17.7 us: pair_gathered(): lax.all_to_all(jnp.broadcast_to(block[None], (2, *block.shape)), 'group',...]
    scatter-add x1 -> x0, other arithmetic: 42.1 us -> none  [body(): jax.ops.segment_sum(returned, served_flat, num_segments=segment_count)]
    all_gather x0 -> x1, blocking collectives: none -> 33.8 us  [body(): lax.all_gather(q_piece, 'local', axis=0, tiled=True)]
    scatter x2 -> x0, local copies, waits for them, and re-layouts: 31.8 us -> none  [the longest x1 19 us: pair_back(): spread = jnp.zeros((vectors_all.shape[0], vectors, vectors), jnp.float32)...]
    dot_general x17 -> x5, matrix products: 31.2 us -> 5.69 us  [the longest x1 2.72 us: body(): jnp.einsum('tbr,rtd->tbd', r_pick, r_low.astype(BF), preferred_element_ty...]
  transfers between devices with their start and end apart: 7 -> 7, of which waited for: 4 -> 6; matrix products, arithmetic and copies ran while one was open for 35% -> 7% of each run, Pallas kernels for 0% -> 9%
where the time goes in v1:
time: 303 us; the launch traced here: 302 us
  waiting for transfers between devices  79.6 us (26%)
  blocking collectives  79 us (26%)
  Pallas kernels  56.2 us (19%)
  starting transfers between devices  30.8 us (10%)
  other arithmetic  24.3 us (8%)
  between operations  14.5 us (5%)
  local copies, waits for them, and re-layouts  11.4 us (4%)
  matrix products  5.69 us (2%)
    all_gather x1, blocking collectives, body(): lax.all_gather(q_piece, 'local', axis=0, tiled=True)  33.8 us
    pallas_call x1, Pallas kernels, compute(): pl.pallas_call(compute_kernel, out_shape=(shape((GROUPS, CAP, DIM), BF),...  27.2 us
    all_to_all x1, waiting for transfers between devices, body(): lax.all_to_all(half, BOTH, 0, 0, tiled=True, axis_index_groups=SAME_CORE_...  26.5 us
    all_to_all x2, blocking collectives, pair_gathered(): lax.all_to_all(jnp.broadcast_to(block[None], (2, *block.shape)), 'group',...  17.7 us
    all_to_all x1, waiting for transfers between devices, body(): returned = lax.all_to_all(outbound, 'group', 0, 0, tiled=True)  17.7 us
    pallas_call x1, Pallas kernels, segment_rows(): call(segment_kernel, jax.ShapeDtypeStruct((LOOKUPS, DIM), BF), [smem(), v...  17.6 us
    all_to_all x1, blocking collectives, body(): request = lax.all_to_all(outgoing, 'group', 0, 0, tiled=True)  16.6 us
    all_to_all x1, blocking collectives, pair_summed(): lax.all_to_all(blocks, 'group', 0, 0, tiled=True, axis_index_groups=CORE_...  10.9 us
  transfers between devices with their start and end apart: 7, of which 6 were waited for; matrix products, arithmetic and copies ran while one was open for 7% of the time, Pallas kernels for 9%

profile of v1, /device:TPU:1, one launch (start us, length us, event | category | flops | bytes accessed | tf_op | source)
XLA Modules:
  0.0 301.5 jit_solution(2632830736969088631)
XLA Ops:
  7.2 0.0 all-gather.2.cloned.1.call-start
  7.2 0.7 all-gather.2.cloned.1.call-update
  7.9 0.7 copy.36
  8.6 0.2 convert_reduce_fusion
  8.8 0.1 fusion.27
  9.0 0.3 fusion.14
  9.3 0.7 convert_bitcast_fusion
  10.0 0.1 fusion.22
  10.1 0.6 fusion.16
  10.8 16.6 %all_to_all.56 = s32[32,1,208]{2,1,0:T(1,128)S(1)} all-to-all(s32[32,1,208]{2,1,0:T(1,128)S(1)} %copy.28), channel_id=1, replica_groups=mesh['group'=32,'local'=4] {'group'}, dimensions={0} | all-to-all | bytes 53248 | tf_op jit(solution)/shard_map/all_to_all | solution.py:454
  27.4 9.5 %serve_rows.1 = bf16[32,208,128]{2,1,0:T(8,128)(2,1)} custom-call(s32[32,208]{1,0:T(8,128)S(1)} %bitcast.56, f32[3328,128]{1,0:T(8,128)S(1)} %bitcast.55), custom_call_target="tpu_custom_call" | custom-call | tf_op jit(solution)/shard_map/serve_rows/pallas_call | solution.py:66
  37.0 4.8 %all-to-all-start.1 = ((bf16[32,208,128]{2,1,0:T(8,128)(2,1)}), bf16[32,208,128]{2,1,0:T(8,128)(2,1)}, u32[]{:S(2)}, u32[]{:S(2)}) async-start(bf16[32,208,128]{2,1,0:T(8,128)(2,1)} %serve_rows.1), calls=%async_computation.1 | async-start | bytes 3407872 | tf_op jit(solution)/shard_map/all_to_all | solution.py:457
  41.8 0.0 copy-start.23
  41.9 0.1 pad.4.w_one
  42.0 1.0 fusion.10.select
  43.0 1.0 fusion.11.mirror
  44.0 10.3 %all-gather.2.cloned.1.call-done = f32[256,26,128]{2,0,1:T(8,128)} async-done(((f32[64,26,128]{2,0,1:T(8,128)}), f32[256,26,128]{2,0,1:T(8,128)}) %all-gather.2.cloned.1.call-update) | async-done | bytes 3407888 | tf_op jit(solution)/shard_map/all_gather | solution.py:459
  54.4 2.7 fusion.1
  57.1 0.3 copy-done.15
  57.4 0.0 copy-start.13
  57.4 0.0 copy-start.14
  57.4 1.9 fusion.8.r_rows
  59.3 7.1 %all-to-all-done.1.arrived = bf16[32,208,128]{2,1,0:T(8,128)(2,1)} async-done(((bf16[32,208,128]{2,1,0:T(8,128)(2,1)}), bf16[32,208,128]{2,1,0:T(8,128)(2,1)}, u32[]{:S(2)}, u32[]{:S(2)}) %all-to-all-start.1) | async-done | bytes 1703968 | tf_op jit(solution)/shard_map/all_to_all | solution.py:457
  66.5 1.4 copy-done.3
  67.9 1.2 copy-done.4
  69.2 1.1 copy-done.6
  70.3 1.1 copy-done.7
  71.4 0.8 copy-done.11
  72.1 27.2 %compute_step.1 = (bf16[32,208,128]{2,1,0:T(8,128)(2,1)S(1)}, bf16[128,512]{1,0:T(8,128)(2,1)S(1)}, bf16[128,1024]{1,0:T(8,128)(2,1)S(1)}, bf16[128,1024]{1,0:T(...) custom-call(s32[26,128]{1,0:T(8,128)S(1)} %multiply_add_fusion.posit, ...), custom_call_target="tpu_custom_call" | custom-call | tf_op jit(solution)/shard_map/compute_step/pallas_call | solution.py:244
  99.4 1.8 weight_grads.1
  101.2 10.9 %all_to_all.57 = bf16[2,512,3072]{2,1,0:T(8,128)(2,1)} all-to-all(bf16[2,512,3072]{2,1,0:T(8,128)(2,1)S(1)} %bitcast.54), channel_id=1, replica_groups={{0,4},{8,12},{16,20},{24,28},{32,36},{40,44},{48,52},{56,60},{64,68},{7..., dimensions={0} | all-to-all | bytes 12582912 | tf_op jit(solution)/shard_map/all_to_all | solution.py:405
  112.1 4.7 %all-to-all-start.2 = ((bf16[32,208,128]{2,1,0:T(8,128)(2,1)}), bf16[32,208,128]{2,1,0:T(8,128)(2,1)}, u32[]{:S(2)}, u32[]{:S(2)}) async-start(bf16[32,208,128]{2,1,0:T(8,128)(2,1)} %copy-done.8), calls=%async_computation.2 | async-start | bytes 3407872 | tf_op jit(solution)/shard_map/all_to_all | solution.py:491
  116.8 6.7 %reduce_sum.57 = bf16[512,3072]{1,0:T(8,128)(2,1)} reduce(bf16[2,512,3072]{2,1,0:T(8,128)(2,1)} %all_to_all.57, bf16[]{:T(256)} %constant.8.clone.1), dimensions={0}, to_apply=%region_3.4 | reduce | flops 1572864 | bytes 9437186 | tf_op jit(solution)/shard_map/reduce_sum | solution.py:400
  123.5 17.7 %all-to-all-done.2.returned = bf16[32,208,128]{2,1,0:T(8,128)(2,1)} async-done(((bf16[32,208,128]{2,1,0:T(8,128)(2,1)}), bf16[32,208,128]{2,1,0:T(8,128)(2,1)}, u32[]{:S(2)}, u32[]{:S(2)}) %all-to-all-start.2) | async-done | bytes 1703968 | tf_op jit(solution)/shard_map/all_to_all | solution.py:491
  141.2 7.6 %all-to-all-start.5 = ((bf16[64,8,3072]{2,1,0:T(8,128)(2,1)}), bf16[64,8,3072]{2,1,0:T(8,128)(2,1)}, u32[]{:S(2)}, u32[]{:S(2)}) async-start(bf16[64,8,3072]{2,1,0:T(8,128)(2,1)} %bitcast.65), calls=%async_computation.5 | async-start | bytes 6291456 | tf_op jit(solution)/shard_map/all_to_all | solution.py:496
  148.8 17.6 %segment_rows.1 = bf16[3328,128]{1,0:T(8,128)(2,1)} custom-call(s32[32,208]{1,0:T(8,128)S(1)} %bitcast.57, bf16[32,208,128]{2,1,0:T(8,128)(2,1)} %all-to-all-done.2.returned), custom_call_target="tpu_custom_call" | custom-call | tf_op jit(solution)/shard_map/segment_rows/pallas_call | solution.py:380
  166.4 26.5 %all-to-all-done.5 = bf16[64,8,3072]{2,1,0:T(8,128)(2,1)} async-done(((bf16[64,8,3072]{2,1,0:T(8,128)(2,1)}), bf16[64,8,3072]{2,1,0:T(8,128)(2,1)}, u32[]{:S(2)}, u32[]{:S(2)}) %all-to-all-start.5) | async-done | bytes 3145760 | tf_op jit(solution)/shard_map/all_to_all | solution.py:496
  192.9 3.5 %all-to-all-start.3 = ((bf16[4,832,128]{2,1,0:T(8,128)(2,1)}), bf16[4,832,128]{2,1,0:T(8,128)(2,1)S(1)}, u32[]{:S(2)}, u32[]{:S(2)}) async-start(bf16[4,832,128]{2,1,0:T(8,128)(2,1)} %bitcast.12), calls=%async_computation.3 | async-start | bytes 1703936 | tf_op jit(solution)/shard_map/all_to_all | solution.py:521
  196.4 2.3 reduce_sum.58
  198.8 10.0 %all-to-all-done.3 = bf16[4,832,128]{2,1,0:T(8,128)(2,1)S(1)} async-done(((bf16[4,832,128]{2,1,0:T(8,128)(2,1)}), bf16[4,832,128]{2,1,0:T(8,128)(2,1)S(1)}, u32[]{:S(2)}, u32[]{:S(2)}) %all-to-all-start.3) | async-done | bytes 852000 | tf_op jit(solution)/shard_map/all_to_all | solution.py:521
  208.8 0.7 broadcast_in_dim.22
  209.5 4.6 %all-to-all-start.6 = ((bf16[16,8,896]{2,1,0:T(8,128)(2,1)}), bf16[16,8,896]{2,1,0:T(8,128)(2,1)S(1)}, u32[]{:S(2)}, u32[]{:S(2)}) async-start(bf16[16,8,896]{2,1,0:T(8,128)(2,1)} %broadcast_in_dim.22), calls=%async_computation.6 | async-start | bytes 458752 | tf_op jit(solution)/shard_map/all_to_all | solution.py:507
  214.1 7.4 %all-to-all-done.6 = bf16[16,8,896]{2,1,0:T(8,128)(2,1)S(1)} async-done(((bf16[16,8,896]{2,1,0:T(8,128)(2,1)}), bf16[16,8,896]{2,1,0:T(8,128)(2,1)S(1)}, u32[]{:S(2)}, u32[]{:S(2)}) %all-to-all-start.6) | async-done | bytes 229408 | tf_op jit(solution)/shard_map/all_to_all | solution.py:507
  221.5 7.5 %all_to_all.58 = bf16[2,16,8,896]{3,2,1,0:T(8,128)(2,1)} all-to-all(bf16[2,16,8,896]{3,2,1,0:T(8,128)(2,1)S(1)} %broadcast_in_dim.23), channel_id=1, replica_groups={{0,4},{8,12},{16,20},{24,28},{32,36},{40,44},{48,52},{56,60},{64,68},{7..., dimensions={0} | all-to-all | bytes 917504 | tf_op jit(solution)/shard_map/all_to_all | solution.py:410
  229.0 1.5 broadcast_in_dim.24
  230.5 5.5 %all-to-all-start.8 = ((bf16[64,8,2176]{2,1,0:T(8,128)(2,1)}), bf16[64,8,2176]{2,1,0:T(8,128)(2,1)}, u32[]{:S(2)}, u32[]{:S(2)}) async-start(bf16[64,8,2176]{2,1,0:T(8,128)(2,1)} %broadcast_in_dim.24), calls=%async_computation.8 | async-start | bytes 4456448 | tf_op jit(solution)/shard_map/all_to_all | solution.py:498
  236.0 0.2 reduce_sum.56
  236.2 33.8 %all_gather.7 = bf16[3328,128]{1,0:T(8,128)(2,1)S(1)} all-gather(bf16[832,128]{1,0:T(8,128)(2,1)S(1)} %reduce_sum.56), channel_id=1, replica_groups=mesh['group'=32,'local'=4] {'local'}, dimensions={0}, use_global_device_ids=true | all-gather | bytes 1064960 | tf_op jit(solution)/shard_map/all_gather | solution.py:523
  270.0 0.1 convert_multiply_fusion
  270.2 1.4 sub.34
  271.6 0.3 copy-done.19
  271.9 1.0 bitcast_subtract_fusion
  272.9 1.9 broadcast_in_dim.26
  274.8 10.2 %all_to_all.59 = bf16[2,512,2176]{2,1,0:T(8,128)(2,1)S(1)} all-to-all(bf16[2,512,2176]{2,1,0:T(8,128)(2,1)S(1)} %broadcast_in_dim.26), channel_id=1, replica_groups={{0,4},{8,12},{16,20},{24,28},{32,36},{40,44},{48,52},{56,60},{64,68},{7..., dimensions={0} | all-to-all | bytes 8912896 | tf_op jit(solution)/shard_map/all_to_all | solution.py:410
  285.1 0.1 fusion.30
  285.2 0.3 maximum_convert_fusion
  285.5 2.7 multiply_subtract_fusion
  288.2 1.7 multiply_subtract_fusion.1
  289.9 0.6 sub.41
  290.5 0.6 sub.37
  291.0 0.6 sub.39
  291.6 1.6 fusion.4
  293.3 0.6 sub.43
  293.8 0.9 multiply_subtract_fusion.2
  (57 shorter events, 0.3 us)
Async XLA Ops:
  7.2 20.3 %copy-start.1 = (f32[128,26,128]{2,0,1:T(8,128)S(1)}, f32[128,26,128]{2,0,1:T(8,128)}, u32[]{:S(2)}) copy-start(f32[128,26,128]{2,0,1:T(8,128)} %param.18) | copy-start | bytes 5111812
  7.2 47.2 %all-gather.2.cloned.1.call-start = ((), (), s32[]{:S(2)}) async-start(), calls=%async_computation.10 | async-start | bytes 4259840 | tf_op jit(solution)/shard_map/all_gather | solution.py:459
  36.9 4.9 %copy-start.20 = (s32[128,26]{0,1:T(8,128)S(1)}, s32[128,26]{0,1:T(8,128)}, u32[]{:S(2)}) copy-start(s32[128,26]{0,1:T(8,128)} %param.22) | copy-start | bytes 39940
  37.0 4.9 %copy-start.16 = (bf16[479,1024]{1,0:T(8,128)(2,1)S(1)}, bf16[479,1024]{1,0:T(8,128)(2,1)}, u32[]{:S(2)}) copy-start(bf16[479,1024]{1,0:T(8,128)(2,1)} %param.23) | copy-start | bytes 2942980
  37.0 5.0 %copy-start.22 = (s32[128,26,1]{0,2,1:T(1,128)S(1)}, s32[128,26,1]{0,2,1:T(1,128)}, u32[]{:S(2)}) copy-start(s32[128,26,1]{0,2,1:T(1,128)} %param.20) | copy-start | bytes 39940
  37.0 5.0 %copy-start.24 = (s32[896]{0:T(1024)S(1)}, s32[896]{0:T(1024)}, u32[]{:S(2)}) copy-start(s32[896]{0:T(1024)} %constant.14.clone) | copy-start | bytes 10756
  37.0 29.5 %all-to-all-start.1 = ((bf16[32,208,128]{2,1,0:T(8,128)(2,1)}), bf16[32,208,128]{2,1,0:T(8,128)(2,1)}, u32[]{:S(2)}, u32[]{:S(2)}) async-start(bf16[32,208,128]{2,1,0:T(8,128)(2,1)} %serve_rows.1), calls=%async_computation.1 | async-start | bytes 3407872 | tf_op jit(solution)/shard_map/all_to_all | solution.py:457
  41.8 1.2 copy-start.23
  54.4 3.0 copy-start.15
  54.4 3.0 copy-start.21
  57.3 9.1 %copy-start = (bf16[1024,1024]{1,0:T(8,128)(2,1)S(1)}, bf16[1024,1024]{1,0:T(8,128)(2,1)}, u32[]{:S(2)}) copy-start(bf16[1024,1024]{1,0:T(8,128)(2,1)} %w_two.1) | copy-start | bytes 6291460
  57.3 9.1 %copy-start.9 = (bf16[512,256]{1,0:T(8,128)(2,1)S(1)}, bf16[512,256]{1,0:T(8,128)(2,1)}, u32[]{:S(2)}) copy-start(bf16[512,256]{1,0:T(8,128)(2,1)} %w_four.1) | copy-start | bytes 786436
  57.3 9.1 %copy-start.10 = (bf16[128,256]{1,0:T(8,128)(2,1)S(1)}, bf16[128,256]{1,0:T(8,128)(2,1)}, u32[]{:S(2)}) copy-start(bf16[128,256]{1,0:T(8,128)(2,1)} %cot.3) | copy-start | bytes 196612
  57.4 9.1 %copy-start.12 = (f32[1024]{0:T(1024)S(1)}, f32[1024]{0:T(1024)}, u32[]{:S(2)}) copy-start(f32[1024]{0:T(1024)} %param.24) | copy-start | bytes 12292
  57.4 9.1 %copy-start.13 = (f32[1024]{0:T(1024)S(1)}, f32[1024]{0:T(1024)}, u32[]{:S(2)}) copy-start(f32[1024]{0:T(1024)} %param.26) | copy-start | bytes 12292
  57.4 9.1 %copy-start.14 = (f32[512]{0:T(512)S(1)}, f32[512]{0:T(512)}, u32[]{:S(2)}) copy-start(f32[512]{0:T(512)} %param.28) | copy-start | bytes 6148
  66.5 1.5 copy-start.3
  67.9 1.2 copy-start.4
  69.2 1.1 copy-start.6
  70.3 1.1 copy-start.7
  71.4 0.8 copy-start.11
  99.4 1.8 copy-start.8
  112.1 29.1 %all-to-all-start.2 = ((bf16[32,208,128]{2,1,0:T(8,128)(2,1)}), bf16[32,208,128]{2,1,0:T(8,128)(2,1)}, u32[]{:S(2)}, u32[]{:S(2)}) async-start(bf16[32,208,128]{2,1,0:T(8,128)(2,1)} %copy-done.8), calls=%async_computation.2 | async-start | bytes 3407872 | tf_op jit(solution)/shard_map/all_to_all | solution.py:491
  141.2 51.7 %all-to-all-start.5 = ((bf16[64,8,3072]{2,1,0:T(8,128)(2,1)}), bf16[64,8,3072]{2,1,0:T(8,128)(2,1)}, u32[]{:S(2)}, u32[]{:S(2)}) async-start(bf16[64,8,3072]{2,1,0:T(8,128)(2,1)} %bitcast.65), calls=%async_computation.5 | async-start | bytes 6291456 | tf_op jit(solution)/shard_map/all_to_all | solution.py:496
  192.9 15.8 %all-to-all-start.3 = ((bf16[4,832,128]{2,1,0:T(8,128)(2,1)}), bf16[4,832,128]{2,1,0:T(8,128)(2,1)S(1)}, u32[]{:S(2)}, u32[]{:S(2)}) async-start(bf16[4,832,128]{2,1,0:T(8,128)(2,1)} %bitcast.12), calls=%async_computation.3 | async-start | bytes 1703936 | tf_op jit(solution)/shard_map/all_to_all | solution.py:521
  209.5 12.0 %all-to-all-start.6 = ((bf16[16,8,896]{2,1,0:T(8,128)(2,1)}), bf16[16,8,896]{2,1,0:T(8,128)(2,1)S(1)}, u32[]{:S(2)}, u32[]{:S(2)}) async-start(bf16[16,8,896]{2,1,0:T(8,128)(2,1)} %broadcast_in_dim.22), calls=%async_computation.6 | async-start | bytes 458752 | tf_op jit(solution)/shard_map/all_to_all | solution.py:507
  230.5 42.4 %all-to-all-start.8 = ((bf16[64,8,2176]{2,1,0:T(8,128)(2,1)}), bf16[64,8,2176]{2,1,0:T(8,128)(2,1)}, u32[]{:S(2)}, u32[]{:S(2)}) async-start(bf16[64,8,2176]{2,1,0:T(8,128)(2,1)} %broadcast_in_dim.24), calls=%async_computation.8 | async-start | bytes 4456448 | tf_op jit(solution)/shard_map/all_to_all | solution.py:498
  236.2 34.0 %copy-start.2 = (f32[128,26,128]{2,0,1:T(8,128)S(1)}, f32[128,26,128]{2,0,1:T(8,128)}, u32[]{:S(2)}) copy-start(f32[128,26,128]{2,0,1:T(8,128)} %param.18) | copy-start | bytes 5111812
  270.2 1.4 copy-start.18
  270.2 1.7 copy-start.19
  285.5 2.7 copy-start.5
  288.2 3.4 %copy-start.17 = (bf16[479,1024]{1,0:T(8,128)(2,1)S(1)}, bf16[479,1024]{1,0:T(8,128)(2,1)}, u32[]{:S(2)}) copy-start(bf16[479,1024]{1,0:T(8,128)(2,1)} %param.23) | copy-start | bytes 2942980
  291.6 1.6 copy-start.25
Sparse Core Ops, SparseCore 0:
  9.7 44.6 all-gather.1
